TPU v7x, 16 devices: a whole 2x2x2 slice. The times are simulated.
16 devices in a mesh: dp: 1, sp: 16 (over x, y, z, core).
Axes of the slice: x: 2, y: 2, z: 2, core: 2. Of those that a mesh axis runs over, the one named last changes fastest.
Arguments:
- q: bfloat16 [32, 96, 192], P('dp')
- k: bfloat16 [32, 8192, 8, 192], P('dp', 'sp')
- v: bfloat16 [32, 8192, 8, 192], P('dp', 'sp')
Outputs:
- q: bfloat16 [32, 96, 192], P('dp')
All inputs are finite; a program needn't handle non-finite values.
Results may differ from a plain program's by a relative error of at most 0.012.
Values are sent between devices in bfloat16 or wider.
A program may use at most 2 GiB of HBM per device.

v0:
```python
import jax
import jax.numpy as jnp
from jax import lax
from jax.sharding import PartitionSpec as P


def einsum(form, a, b):
    return jnp.einsum(form, a.astype(jnp.float32), b.astype(jnp.float32))


def part_of(q, k, v):
    grouped = q.reshape(q.shape[0], k.shape[2], -1, q.shape[2])
    scores = einsum("bgsd,bugd->bgsu", grouped, k) * q.shape[2] ** -0.5
    high = jnp.max(scores, -1, keepdims=True)
    weights = jnp.exp(scores - high)
    seen = einsum("bgsu,bugd->bgsd", weights.astype(jnp.bfloat16), v)
    return jnp.concatenate([seen, jnp.sum(weights, -1, keepdims=True), high], -1)


def together(parts):
    seen, total, high = parts[..., :-2], parts[..., -2:-1], parts[..., -1:]
    scale = jnp.exp(high - jnp.max(high, 0))
    return (jnp.sum(seen * scale, 0) / jnp.sum(total * scale, 0)).astype(jnp.bfloat16)


def solution(mesh):
    def step(q, k, v):
        return together(lax.all_gather(part_of(q, k, v), "sp")).reshape(q.shape)

    return jax.shard_map(
        step,
        mesh=mesh,
        in_specs=(P("dp", None, None), P("dp", "sp", None, None), P("dp", "sp", None, None)),
        out_specs=P("dp", None, None),
        check_vma=False,
    )
```

profile of v0, /device:TPU:0, one launch (start us, length us, event | category | flops | bytes accessed | tf_op | source)
XLA Modules:
  0.0 362.5 jit_solution(4252191252637862938)
XLA Ops:
  6.5 0.0 all-gather.3.cloned.1.call-start
  6.5 2.3 copy.38
  8.8 17.8 %multiply_reduce_fusion = (f32[32,8,12]{2,1,0:T(8,128)S(1)}, f32[32,8,12,512]{3,2,1,0:T(8,128)S(1)}) fusion(bf16[32,512,8,192]{1,3,2,0:T(8,128)(2,1)} %param.4, bf16[32,8,12,192]{3,0,2,1:T(8,128)(2,1)S(1)} %bitcast.16), kind=kOutput, calls=%fused_computation.3 | convolution fusion | flops 607122432 | bytes 57815040 | tf_op jit(solution)/shard_map/bgsd,bugd->bgsu/dot_general | solution.py:8
  26.7 0.0 copy-start
  26.7 3.2 copy-done
  29.9 2.2 fusion.1
  32.2 23.8 %fusion.3 = f32[32,8,12,192]{3,2,1,0:T(8,128)} fusion(bf16[32,512,8,192]{1,3,2,0:T(8,128)(2,1)} %param.5, f32[32,8,12,512]{3,2,1,0:T(8,128)} %copy-done, f32[32,8,12]{2,1,0:T(8,128)S(1)} %get-tuple-element.10), kind=kOutput, calls=%fused_computation.6 | convolution fusion | flops 608698368 | bytes 58994688 | tf_op jit(solution)/shard_map/bgsu,bugd->bgsd/dot_general | solution.py:8
  55.9 1.7 copy.42
  57.6 3.0 copy.43
  60.6 4.1 %pad_maximum_fusion = f32[32,8,12,194]{3,2,1,0:T(8,128)S(1)} fusion(f32[32,8,12,1]{3,2,1,0:T(8,128)} %copy.43, f32[32,8,12,1]{3,2,1,0:T(8,128)S(1)} %copy.42, f32[32,8,12,192]{3,2,1,0:T(8,128)} %fusion.3), kind=kLoop, calls=%fused_computation.7 | loop fusion | flops 1191936 | bytes 4767744 | tf_op jit(solution)/shard_map/concatenate | solution.py:17
  64.7 4.5 %copy.44 = f32[32,8,12,194]{3,1,2,0:T(8,128)} copy(f32[32,8,12,194]{3,2,1,0:T(8,128)S(1)} %pad_maximum_fusion) | data formatting | bytes 4767744 | tf_op jit(solution)/shard_map/concatenate | solution.py:17
  69.2 0.0 all-gather.3.cloned.1.call-update
  69.2 189.1 %all-gather.3.cloned.1.call-done = f32[512,8,12,194]{3,1,2,0:T(8,128)} async-done(((f32[32,8,12,194]{3,1,2,0:T(8,128)}), f32[512,8,12,194]{3,1,2,0:T(8,128)}) %all-gather.3.cloned.1.call-update) | async-done | bytes 38141968 | tf_op jit(solution)/shard_map/all_gather | solution.py:28
  258.4 36.8 %fusion.12 = (f32[16,32,8,12,1]{4,2,3,1,0:T(8,128)}, f32[32,8,12]{1,2,0:T(8,128)S(1)}, f32[16,32,8,12,1]{4,2,3,1,0:T(8,128)}) fusion(f32[16,32,8,12,194]{4,2,3,1,0:T(8,128)} %bitcast.14), kind=kLoop, calls=%fused_computation.19 | loop fusion | flops 46080 | bytes 798720 | tf_op jit(solution)/shard_map/slice | solution.py:21
  295.2 17.2 %copy.58 = f32[16,32,8,12,1]{1,2,4,3,0:T(8,128)S(1)} copy(f32[16,32,8,12,1]{4,2,3,1,0:T(8,128)} %get-tuple-element.5) | data formatting | bytes 393216
  312.4 0.1 copy.60
  312.6 17.2 %copy.57 = f32[16,32,8,12,1]{1,2,4,3,0:T(8,128)S(1)} copy(f32[16,32,8,12,1]{4,2,3,1,0:T(8,128)} %get-tuple-element.7) | data formatting | bytes 393216
  329.8 0.2 multiply_reduce_fusion.1
  330.0 2.9 copy.46
  332.9 18.3 %fusion = f32[32,8,12,192]{3,1,2,0:T(8,128)S(1)} fusion(f32[16,32,8,12,194]{4,2,3,1,0:T(8,128)} %bitcast.15, f32[16,32,8,12]{2,3,1,0:T(8,128)} %copy.46), kind=kLoop, calls=%fused_computation.1 | loop fusion | flops 18284544 | bytes 40304640 | tf_op jit(solution)/shard_map/reduce_sum | solution.py:23
  351.3 1.8 copy.48
  353.1 0.5 fusion.7
  353.6 2.0 copy.51
  (2 shorter events, 0.0 us)
Async XLA Ops:
  6.5 251.8 %all-gather.3.cloned.1.call-start = ((), (), s32[]{:S(2)}) async-start(), calls=%async_computation | async-start | bytes 53477376 | tf_op jit(solution)/shard_map/all_gather | solution.py:28
  26.7 3.2 copy-start
Sparse Core Ops, SparseCore 0:
  69.4 188.9 all-gather.2
where the time goes:
time: 363 us; the launch traced here: 362 us
  waiting for transfers between devices  189 us (52%)
  other arithmetic  62.2 us (17%)
  local copies, waits for them, and re-layouts  56.1 us (15%)
  matrix products  41.6 us (11%)
  between operations  13.5 us (4%)
    all_gather x1, waiting for transfers between devices, step(): return together(lax.all_gather(part_of(q, k, v), 'sp')).reshape(q.shape)  189 us
    dot_general x2, matrix products, einsum(): return jnp.einsum(form, a.astype(jnp.float32), b.astype(jnp.float32))  41.6 us
    unnamed x6, local copies, waits for them, and re-layouts  40.1 us
    slice x1, other arithmetic, together(): seen, total, high = (parts[..., :-2], parts[..., -2:-1], parts[..., -1:])  36.8 us
    reduce_sum x1, other arithmetic, together(): jnp.sum(seen * scale, 0) / jnp.sum(total * scale, 0)  18.3 us
  transfers between devices with their start and end apart: 1, of which 1 were waited for; matrix products, arithmetic and copies ran while one was open for 0% of the time, Pallas kernels for 0%

commit v1 on v0

v1 whole, which is shorter than its diff:
```python
import functools
import math

import jax
import jax.numpy as jnp
from jax import lax
from jax.experimental import pallas as pl
from jax.experimental.pallas import tpu as pltpu
from jax.sharding import PartitionSpec as P

MESH = pl.DeviceIdType.MESH
RING = 4


def wait_for(ref, sem):
    pltpu.make_async_copy(ref, ref, sem).wait()


def kernel(
    scale,
    q_hbm,
    k_hbm,
    v_hbm,
    out,
    q,
    kbuf,
    vbuf,
    scores,
    highs,
    mine,
    mine_st,
    other,
    other_st,
    part,
    part_st,
    sums,
    stats,
    q_sem,
    k_sem,
    v_sem,
    d_send,
    d_recv,
    dst_send,
    dst_recv,
    s_send,
    s_recv,
    st_send,
    st_recv,
    rel_send,
    rel_recv,
):
    pairs = k_hbm.shape[0] // 2
    me = lax.axis_index("sp")
    core = me % 2
    partner = me + 1 - 2 * core
    bits = [me // 8, (me // 4) % 2, (me // 2) % 2]
    peers = [me + n - 2 * n * bit for n, bit in zip((8, 4, 2), bits)]
    lane = lax.broadcasted_iota(jnp.int32, (8, 128), 1)
    row = lax.broadcasted_iota(jnp.int32, (8, 128), 0)
    spot = [lane == row + 8 * k for k in range(12)]
    row_low = lax.broadcasted_iota(jnp.int32, (8, 512), 0) < 4
    lane_low = lane < 64
    power = scale * math.log2(math.e)

    def seq(p, j):
        return 2 * p + (1 - core) + j * (2 * core - 1)

    def k_copy(p, j):
        slot = 2 * (p % RING) + j
        return pltpu.make_async_copy(k_hbm.at[seq(p, j)], kbuf.at[slot], k_sem.at[slot])

    def v_copy(p, j):
        slot = 2 * (p % RING) + j
        return pltpu.make_async_copy(v_hbm.at[seq(p, j)], vbuf.at[slot], v_sem.at[slot])

    def send(src, dst, ssem, rsem, to):
        pltpu.make_async_remote_copy(
            src_ref=src, dst_ref=dst, send_sem=ssem, recv_sem=rsem, device_id={"sp": to}, device_id_type=MESH
        ).start()

    def factors(a, b, last):
        high = jnp.maximum(a[:1], b[:1])
        fa, fb = jnp.exp2((a[:1] - high) * power), jnp.exp2((b[:1] - high) * power)
        total = fa * a[1:] + fb * b[1:]
        if last:
            fa, fb = fa / total, fb / total

        def columns(f):
            f = jnp.broadcast_to(f, (8, 128))
            c = [jnp.sum(jnp.where(here, f, 0.0), 1, keepdims=True) for here in spot]
            return c + [jnp.where(lane_low, c[k], c[k + 6]) for k in range(6)]

        return columns(fa), columns(fb), jnp.concatenate([high, total], 0)

    def added(a, b, fa, fb):
        return [
            a[8 * k : 8 * k + 8].astype(jnp.float32) * fa[k] + b[8 * k : 8 * k + 8].astype(jnp.float32) * fb[k]
            for k in range(18)
        ]

    def slot_of(p):
        if isinstance(p, int):
            return p if 0 <= p < pairs else pairs
        return jnp.where(p >= 0, p, pairs)

    def add(p, s):
        n = slot_of(p)
        if s == 0:
            a, b, sa, sb = mine[n % 4], part[n], mine_st[n % 4], part_st[n]
        else:
            a, b, sa, sb = sums[s - 1, n, 0], sums[s - 1, n, 1], stats[s - 1, n, 0], stats[s - 1, n, 1]
        fa, fb, st = factors(sa, sb, s == 3)
        tiles = added(a, b, fa, fb)
        if s < 3:
            sums[s, n, bits[s]] = jnp.concatenate(tiles, 0).astype(jnp.bfloat16)
            stats[s, n, bits[s]] = st
            return
        b = seq(max(p, 0) if isinstance(p, int) else jnp.where(p >= 0, p, 0), 1)
        out[b, :, :128] = jnp.concatenate(tiles[:12], 0).astype(out.dtype)
        rest = jnp.concatenate(tiles[12:], 0)
        out[b, :48, 128:] = rest[:, :64].astype(out.dtype)
        out[b, 48:, 128:] = rest[:, 64:].astype(out.dtype)

    def start(p, s):
        if s == 0:
            send(other.at[p], part.at[p], d_send.at[p], d_recv.at[p], partner)
            send(other_st.at[p], part_st.at[p], dst_send.at[p], dst_recv.at[p], partner)
        elif s < 4:
            s = s - 1
            at = (s, p, bits[s])
            send(sums.at[at], sums.at[at], s_send.at[s, p], s_recv.at[s, p], peers[s])
            send(stats.at[at], stats.at[at], st_send.at[s, p], st_recv.at[s, p], peers[s])
        else:
            b = seq(p, 1)
            send(out.at[b], out.at[b], rel_send.at[p], rel_recv.at[p], partner)

    def arrive(p, s):
        if s == 0:
            wait_for(part.at[p], d_recv.at[p])
            wait_for(part_st.at[p], dst_recv.at[p])
        else:
            wait_for(part.at[p], s_recv.at[s - 1, p])
            wait_for(part_st.at[p], st_recv.at[s - 1, p])

    SEND = (2, 4, 7, 10, 13)
    ADD = (3, 6, 9, 12)

    def keys(p):
        for j in range(2):
            b = seq(p, j)
            slot = 2 * (p % RING) + j
            srow = 2 * (p % 2) + j
            acc = jnp.zeros((8, 128), jnp.float32)
            for h in range(4):
                low = jnp.dot(q[b, 24 * h : 24 * h + 16], kbuf[slot, 2 * h], preferred_element_type=jnp.float32)
                top = jnp.dot(q[b, 24 * h + 8 : 24 * h + 24], kbuf[slot, 2 * h + 1], preferred_element_type=jnp.float32)
                tiles = (low[:8], jnp.where(row_low, low[8:], top[:8]), top[8:])
                for t, tile in enumerate(tiles):
                    k = 3 * h + t
                    scores[srow, 8 * k : 8 * k + 8] = tile
                    high = jnp.max(tile, 1, keepdims=True)
                    highs[srow, 8 * k : 8 * k + 8] = jnp.broadcast_to(high, (8, 128))
                    acc = jnp.where(spot[k], high, acc)
            st = jnp.sum(acc, 0, keepdims=True)
            if j == 0:
                other_st[p, :1] = st
            else:
                mine_st[p % 4, :1] = st

    def values(p):
        for j in range(2):
            slot = 2 * (p % RING) + j
            srow = 2 * (p % 2) + j
            acc = jnp.zeros((8, 128), jnp.float32)
            rest = []
            for h in range(4):
                tiles = []
                for t in range(3):
                    k = 3 * h + t
                    top = highs[srow, 8 * k : 8 * k + 8, :1]
                    tile = jnp.exp2((scores[srow, 8 * k : 8 * k + 8] - top) * power)
                    acc = jnp.where(spot[k], jnp.sum(tile, 1, keepdims=True), acc)
                    tiles.append(tile)
                first = jnp.concatenate([tiles[0], jnp.where(row_low, tiles[1], 0.0)], 0).astype(jnp.bfloat16)
                second = jnp.concatenate([jnp.where(row_low, 0.0, tiles[1]), tiles[2]], 0).astype(jnp.bfloat16)
                dims = (((1,), (1,)), ((), ()))
                a = lax.dot_general(first, vbuf[slot, 2 * h], dims, preferred_element_type=jnp.float32)
                z = lax.dot_general(second, vbuf[slot, 2 * h + 1], dims, preferred_element_type=jnp.float32)
                seen = jnp.concatenate([a[:8], a[8:] + z[:8], z[8:]], 0)
                rest.append(seen[:, 128:])
                if j == 0:
                    other[p, 24 * h : 24 * h + 24] = seen[:, :128].astype(jnp.bfloat16)
                else:
                    mine[p % 4, 24 * h : 24 * h + 24] = seen[:, :128]
            rest = jnp.concatenate([jnp.concatenate(rest[:2], 0), jnp.concatenate(rest[2:], 0)], 1)
            st = jnp.sum(acc, 0, keepdims=True)
            if j == 0:
                other[p, 96:] = rest.astype(jnp.bfloat16)
                other_st[p, 1:] = st
            else:
                mine[p % 4, 96:] = rest
                mine_st[p % 4, 1:] = st

    q_copy = pltpu.make_async_copy(q_hbm, q, q_sem)
    k_copy(0, 0).start()
    q_copy.start()
    k_copy(0, 1).start()
    for copy, p in ((k_copy, 1), (v_copy, 0), (k_copy, 2), (v_copy, 1)):
        for j in range(2):
            copy(p, j).start()
    barrier = pltpu.get_barrier_semaphore()
    for to in (partner, *peers):
        pl.semaphore_signal(barrier, inc=1, device_id={"sp": to}, device_id_type=MESH)
    q_copy.wait()
    pl.semaphore_wait(barrier, 4)

    def when(condition, what):
        if isinstance(condition, bool):
            if condition:
                what()
        else:
            pl.when(condition)(what)

    def body(u):
        first, last = isinstance(u, int) and u == 0, isinstance(u, int) and u == pairs
        for j in range(2):
            if not last:
                k_copy(u, j).wait()
            if not first:
                v_copy(u - 1, j).wait()

        def more_keys():
            for j in range(2):
                k_copy(u + 3, j).start()

        def more_values():
            for j in range(2):
                v_copy(u + 2, j).start()

        when(u + 3 < pairs, more_keys)
        when(u + 2 < pairs, more_values)
        for s, lag in enumerate(ADD):
            when(u - lag >= 0, lambda: arrive(u - lag, s))
        for s, lag in enumerate(SEND):
            when(u - lag >= 0, lambda: start(u - lag, s))
        if not last:
            keys(u)
        if not first:
            values(u - 1)
        if not first:
            for s, lag in enumerate(ADD):
                add(u - lag, s)

    body(0)
    lax.fori_loop(1, pairs, lambda u, c: (body(u), c)[1], 0)
    body(pairs)

    todo = []
    for p in range(pairs):
        sent = [s for s in range(5) if p + SEND[s] <= pairs]
        done = [s for s in range(4) if p + ADD[s] <= pairs]
        time = 0.0
        if len(sent) == len(done) < 5:
            todo.append((time, p, len(done), False))
        for s in range(len(done), 4):
            time = max(time + (1.2 if s == 0 else 2.7), 0.0) if s >= len(sent) else (p + SEND[s] - pairs) * 1.5 + 2.0
            time = max(time, 0.0)
            todo.append((time, p, s, True))
    for _, p, s, arrives in sorted(todo):
        if arrives:
            arrive(p, s)
            add(p, s)
            start(p, s + 1)
        else:
            start(p, s)
    for p in range(pairs):
        wait_for(out.at[0], rel_recv.at[p])
        wait_for(out.at[0], rel_send.at[p])
        wait_for(part.at[p], d_send.at[p])
        wait_for(part_st.at[p], dst_send.at[p])
        for s in range(3):
            wait_for(part.at[p], s_send.at[s, p])
            wait_for(part_st.at[p], st_send.at[s, p])


def solution(mesh):
    def step(q, k, v):
        seqs, heads, head = q.shape
        tokens, kv = k.shape[1:3]
        pairs, packed = seqs // 2, heads + heads // 2
        kt = jnp.transpose(k, (0, 2, 3, 1))
        vt = jnp.transpose(v, (0, 2, 3, 1))
        f32, bf16 = jnp.float32, jnp.bfloat16
        vm, dma = pltpu.VMEM, pltpu.SemaphoreType.DMA
        anywhere = pl.BlockSpec(memory_space=pl.ANY)
        return pl.pallas_call(
            functools.partial(kernel, head**-0.5),
            out_shape=jax.ShapeDtypeStruct(q.shape, q.dtype),
            in_specs=[anywhere] * 3,
            out_specs=pl.BlockSpec(memory_space=pltpu.VMEM),
            scratch_shapes=[
                vm((seqs, heads, head), bf16),
                vm((2 * RING, kv, head, tokens), bf16),
                vm((2 * RING, kv, head, tokens), bf16),
                vm((4, heads, tokens), f32),
                vm((4, heads, 128), f32),
                vm((4, packed, 128), f32),
                vm((4, 2, 128), f32),
                vm((pairs, packed, 128), bf16),
                vm((pairs, 2, 128), f32),
                vm((pairs + 1, packed, 128), bf16),
                vm((pairs + 1, 2, 128), f32),
                vm((3, pairs + 1, 2, packed, 128), bf16),
                vm((3, pairs + 1, 2, 2, 128), f32),
                dma(()),
                dma((2 * RING,)),
                dma((2 * RING,)),
                *[dma((pairs,))] * 4,
                *[dma((3, pairs))] * 4,
                *[dma((pairs,))] * 2,
            ],
            compiler_params=pltpu.CompilerParams(
                collective_id=0, has_side_effects=True, vmem_limit_bytes=60 << 20
            ),
            name="decode",
        )(q, kt, vt)

    return jax.shard_map(
        step,
        mesh=mesh,
        in_specs=(P("dp", None, None), P("dp", "sp", None, None), P("dp", "sp", None, None)),
        out_specs=P("dp", None, None),
        check_vma=False,
    )
```

time: 363 us -> 55.3 us (0.15)
  waiting for transfers between devices: 189 us -> 0 us
  other arithmetic: 62.2 us -> 0 us
  local copies, waits for them, and re-layouts: 56.1 us -> 2.65 us
  Pallas kernels: 0 us -> 52.5 us
  matrix products: 41.6 us -> 0 us
  between operations: 13.5 us -> 0.01 us
    all_gather x1 -> x0, waiting for transfers between devices: 189 us -> none  [step(): return together(lax.all_gather(part_of(q, k, v), 'sp')).reshape(q.shape)]
    pallas_call x0 -> x1, Pallas kernels: none -> 52.5 us  [step(): pl.pallas_call(functools.partial(kernel, head ** (-0.5)), out_shape=jax.S...]
    dot_general x2 -> x0, matrix products: 41.6 us -> none  [einsum(): return jnp.einsum(form, a.astype(jnp.float32), b.astype(jnp.float32))]
    unnamed x6 -> x1, local copies, waits for them, and re-layouts: 40.1 us -> 2.65 us
    slice x1 -> x0, other arithmetic: 36.8 us -> none  [together(): seen, total, high = (parts[..., :-2], parts[..., -2:-1], parts[..., -1:])]
    reduce_sum x3 -> x0, other arithmetic: 20.7 us -> none  [the longest x1 18.3 us: together(): jnp.sum(seen * scale, 0) / jnp.sum(total * scale, 0)]
    broadcast_in_dim x2 -> x0, local copies, waits for them, and re-layouts: 4.67 us -> none  [the longest x1 3.01 us: part_of(): high = jnp.max(scores, -1, keepdims=True)]
    concatenate x1 -> x0, local copies, waits for them, and re-layouts: 4.47 us -> none  [part_of(): jnp.concatenate([seen, jnp.sum(weights, -1, keepdims=True), high], -1)]
  transfers between devices with their start and end apart: 1 -> 0, of which waited for: 1 -> 0; matrix products, arithmetic and copies ran while one was open for 0% -> 0% of each run, Pallas kernels for 0% -> 0%
where the time goes in v1:
time: 55.3 us; the launch traced here: 55.2 us
  Pallas kernels  52.5 us (95%)
  local copies, waits for them, and re-layouts  2.65 us (5%)
    pallas_call x1, Pallas kernels, step(): pl.pallas_call(functools.partial(kernel, head ** (-0.5)), out_shape=jax.S...  52.5 us
    unnamed x1, local copies, waits for them, and re-layouts  2.65 us

profile of v1, /device:TPU:0, one launch (start us, length us, event | category | flops | bytes accessed | tf_op | source)
XLA Modules:
  0.0 55.2 jit_solution(4486246217335691426)
XLA Ops:
  0.0 52.5 %decode.1 = bf16[32,96,192]{2,1,0:T(8,128)(2,1)} custom-call(bf16[32,96,192]{2,1,0:T(8,128)(2,1)} %q_hbm.1, bf16[32,8,192,512]{3,2,1,0:T(8,128)(2,1)} %bitcast.2, bf16[32,8,192,512]{3,2,1,0:T(8,128)(2,1)} %bitcast.3), custom_call_target="tpu_custom_call" | custom-call | tf_op jit(solution)/shard_map/decode/pallas_call | solution.py:296
  52.5 2.7 %copy.5 = bf16[32,96,192]{2,1,0:T(8,128)(2,1)} copy(bf16[32,96,192]{2,1,0:T(8,128)(2,1)} %decode.1) | data formatting | bytes 2359296

commit v2 on v1

--- a/solution.py
+++ b/solution.py
@@ -223,6 +223,8 @@
 
     def body(u):
         first, last = isinstance(u, int) and u == 0, isinstance(u, int) and u == pairs
+        for s, lag in enumerate(SEND):
+            when(u - lag >= 0, lambda: start(u - lag, s))
         for j in range(2):
             if not last:
                 k_copy(u, j).wait()
@@ -241,8 +243,6 @@
         when(u + 2 < pairs, more_values)
         for s, lag in enumerate(ADD):
             when(u - lag >= 0, lambda: arrive(u - lag, s))
-        for s, lag in enumerate(SEND):
-            when(u - lag >= 0, lambda: start(u - lag, s))
         if not last:
             keys(u)
         if not first:
@@ -295,7 +295,7 @@
         anywhere = pl.BlockSpec(memory_space=pl.ANY)
         return pl.pallas_call(
             functools.partial(kernel, head**-0.5),
-            out_shape=jax.ShapeDtypeStruct(q.shape, q.dtype),
+            out_shape=pltpu.VMEM(q.shape, q.dtype),
             in_specs=[anywhere] * 3,
             out_specs=pl.BlockSpec(memory_space=pltpu.VMEM),
             scratch_shapes=[
@@ -320,7 +320,7 @@
                 *[dma((pairs,))] * 2,
             ],
             compiler_params=pltpu.CompilerParams(
-                collective_id=0, has_side_effects=True, vmem_limit_bytes=60 << 20
+                collective_id=0, has_side_effects=True, vmem_limit_bytes=56 << 20
             ),
             name="decode",
         )(q, kt, vt)

time: 55.3 us -> 52.4 us (0.948)
  local copies, waits for them, and re-layouts: 2.65 us -> 1.15 us
  Pallas kernels: 52.5 us -> 51.2 us
    unnamed x1, local copies, waits for them, and re-layouts: 2.65 us -> 1.15 us
    pallas_call x1, Pallas kernels: 52.5 us -> 51.2 us  [step(): pl.pallas_call(functools.partial(kernel, head ** (-0.5)), out_shape=pltpu...]
where the time goes in v2:
time: 52.4 us; the launch traced here: 52.3 us
  Pallas kernels  51.2 us (98%)
  local copies, waits for them, and re-layouts  1.15 us (2%)
    pallas_call x1, Pallas kernels, step(): pl.pallas_call(functools.partial(kernel, head ** (-0.5)), out_shape=pltpu...  51.2 us
    unnamed x1, local copies, waits for them, and re-layouts  1.15 us

profile of v2, /device:TPU:0, one launch (start us, length us, event | category | flops | bytes accessed | tf_op | source)
XLA Modules:
  0.0 52.3 jit_solution(13403466843752226260)
XLA Ops:
  0.0 51.2 %decode.1 = bf16[32,96,192]{2,1,0:T(8,128)(2,1)S(1)} custom-call(bf16[32,96,192]{2,1,0:T(8,128)(2,1)} %q_hbm.1, bf16[32,8,192,512]{3,2,1,0:T(8,128)(2,1)} %bitcast.2, bf16[32,8,192,512]{3,2,1,0:T(8,128)(2,1)} %bitcast.3), custom_call_target="tpu_custom_call" | custom-call | tf_op jit(solution)/shard_map/decode/pallas_call | solution.py:296
  51.2 1.1 %copy.5 = bf16[32,96,192]{2,1,0:T(8,128)(2,1)} copy(bf16[32,96,192]{2,1,0:T(8,128)(2,1)S(1)} %decode.1) | data formatting | bytes 2359296
